TPU v7x, 32 devices: a whole 2x2x4 slice. The times are simulated.
32 devices in a mesh: cfg: 2 (over x), space: 8 (over z, y), tm: 2 (over core).
Axes of the slice: x: 2, y: 2, z: 4, core: 2. Of those that a mesh axis runs over, the one named last changes fastest.
Arguments:
- vectors: bfloat16 [4, 64, 6, 8192], P(('cfg', 'tm'), 'space'), parts along dimension 0, may hold values from -0.5 to 0.5
- gauge_links: bfloat16 [4, 3, 18, 8192], P(('cfg', 'tm'), None, None, 'space'), parts along dimension 0, may hold values from -3 to 3
- momenta: int32 [8, 3], replicated, may hold values from -2 to 2
- directions: int32 [3], replicated, may hold values from 0 to 2, each once
Outputs:
- elementals: float32 [64, 4, 8, 3, 128], P('space', ('cfg', 'tm')), parts along dimension 1
There are 2 independent parts, one for each index of `cfg`. A program takes and returns all parts, laid end to end along the dimension named above; an argument that names none is the same for every part. Nothing has to cross between parts.
Inputs may be any that keep to these rules, and one draw needn't show every extreme that they name: `momenta`: integer momentum components, in units of 2 pi over the lattice extent. Each of the directions 0, 1, 2 appears once.
All inputs are finite; a program needn't handle non-finite values.
Results may differ from a plain program's by a relative error of at most 0.005.
Values may be sent and summed in bfloat16 or wider, within the bound.
A program may use at most 128 MiB of HBM per device.

v0:
```python
import math

import jax
import jax.numpy as jnp
from jax import lax
from jax.experimental import pallas as pl
from jax.experimental.pallas import tpu as pltpu
from jax.sharding import PartitionSpec as P

LXY = 32
NMOM = 8
NDIR = 3


TWO_PI = 2.0 * math.pi


def with_halo(cells, sides, width):
    for axis, dim in sides:
        count = lax.axis_size(axis)
        head = lax.slice_in_dim(cells, 0, width, axis=dim)
        tail = lax.slice_in_dim(cells, cells.shape[dim] - width, cells.shape[dim], axis=dim)
        cells = jnp.concatenate(
            [
                lax.ppermute(tail, axis, [(i, (i + 1) % count) for i in range(count)]),
                cells,
                lax.ppermute(head, axis, [((i + 1) % count, i) for i in range(count)]),
            ],
            axis=dim,
        )
    return cells


def from_behind(block, axis, distance):
    devices = range(lax.axis_size(axis))
    route = [((i - distance) % len(devices), i) for i in devices]
    return lax.ppermute(block, axis, route)


def apply_link(link, field_f32):
    real_rows = []
    imag_rows = []
    for row_a in range(3):
        link_re = link[0, row_a, 0][None]
        link_im = link[1, row_a, 0][None]
        real_acc = link_re * field_f32[:, 0, 0] - link_im * field_f32[:, 1, 0]
        imag_acc = link_re * field_f32[:, 1, 0] + link_im * field_f32[:, 0, 0]
        for col_b in range(1, 3):
            link_re = link[0, row_a, col_b][None]
            link_im = link[1, row_a, col_b][None]
            real_acc = (
                real_acc + link_re * field_f32[:, 0, col_b] - link_im * field_f32[:, 1, col_b]
            )
            imag_acc = (
                imag_acc + link_re * field_f32[:, 1, col_b] + link_im * field_f32[:, 0, col_b]
            )
        real_rows.append(real_acc)
        imag_rows.append(imag_acc)
    return jnp.stack([jnp.stack(real_rows, axis=1), jnp.stack(imag_rows, axis=1)], axis=1)


def adjoint(link):
    return jnp.stack([jnp.swapaxes(link[0], 0, 1), -jnp.swapaxes(link[1], 0, 1)])


def pack_terms(derivative, eig_count):
    rounded = derivative.astype(jnp.bfloat16)
    rounded_re = rounded[:, 0]
    rounded_im = rounded[:, 1]
    swapped = jnp.stack([rounded_im, -rounded_re], axis=1)
    return jnp.concatenate([rounded, swapped], axis=0).reshape(2 * eig_count, -1)


def phase_angles(momenta, z_offset, depth_planes, z_length):
    z_coord = z_offset + jnp.arange(depth_planes, dtype=jnp.int32)
    y_coord = jnp.arange(LXY, dtype=jnp.int32)
    x_coord = jnp.arange(LXY, dtype=jnp.int32)
    mom_x = momenta[:, 0][:, None, None, None]
    mom_y = momenta[:, 1][:, None, None, None]
    mom_z = momenta[:, 2][:, None, None, None]
    fraction = (mom_x * x_coord[None, None, None, :] % LXY).astype(jnp.float32) / LXY
    fraction = fraction + (mom_y * y_coord[None, None, :, None] % LXY).astype(jnp.float32) / LXY
    fraction = (
        fraction + (mom_z * z_coord[None, :, None, None] % z_length).astype(jnp.float32) / z_length
    )
    return TWO_PI * fraction


def phase_twist(row_block, cosine_table, sine_table):
    vec_re = row_block[:, 0][None]
    vec_im = row_block[:, 1][None]
    cos_b = cosine_table[:, None, None]
    sin_b = sine_table[:, None, None]
    real_part = vec_re * cos_b - vec_im * sin_b
    imag_part = vec_re * sin_b + vec_im * cos_b
    twisted = jnp.stack([real_part, imag_part], axis=2).astype(jnp.bfloat16)
    return twisted.reshape(cosine_table.shape[0] * row_block.shape[0], -1)


def shards_by_plane(vectors, gauge_links, momenta, directions):
    space_count = lax.axis_size("space")
    slab_count = vectors.shape[0]
    eig_local = vectors.shape[1]
    eig_count = eig_local * space_count
    plane_size = LXY * LXY
    depth_planes = gauge_links.shape[3] // plane_size
    blocks = vectors.reshape(slab_count, eig_local, 6, space_count, depth_planes, plane_size)
    regrouped = lax.all_to_all(blocks, "space", split_axis=3, concat_axis=1, tiled=True)
    local_block = regrouped.reshape(slab_count, eig_count, 6, depth_planes, plane_size)
    extended = with_halo(local_block, (("space", 3),), 1)
    z_links = gauge_links[:, 2].reshape(slab_count, 18, depth_planes, plane_size)
    link_below = from_behind(z_links[:, :, depth_planes - 1, :], "space", 1)
    links_below = jnp.concatenate(
        [link_below[:, :, None, :], z_links[:, :, : depth_planes - 1, :]], axis=2
    )
    z_offset = lax.axis_index("space") * depth_planes
    angles = phase_angles(momenta, z_offset, depth_planes, depth_planes * space_count)
    cosine_all = jnp.cos(angles)
    sine_all = jnp.sin(angles)
    slab = 0
    field_f32 = (
        local_block[slab].reshape(eig_count, 2, 3, depth_planes, LXY, LXY).astype(jnp.float32)
    )
    widened_f32 = (
        extended[slab].reshape(eig_count, 2, 3, depth_planes + 2, LXY, LXY).astype(jnp.float32)
    )
    slab_links = gauge_links[slab].reshape(3, 2, 3, 3, depth_planes, LXY, LXY).astype(jnp.float32)
    prev_links = links_below[slab].reshape(2, 3, 3, depth_planes, LXY, LXY).astype(jnp.float32)
    per_dir = []
    for dir_index, roll_axis in ((0, -1), (1, -2)):
        forward = apply_link(slab_links[dir_index], jnp.roll(field_f32, -1, axis=roll_axis))
        backward = jnp.roll(
            apply_link(adjoint(slab_links[dir_index]), field_f32), 1, axis=roll_axis
        )
        per_dir.append(pack_terms(0.5 * (forward - backward), eig_count))
    forward = apply_link(slab_links[2], widened_f32[:, :, :, 2:])
    backward = apply_link(adjoint(prev_links), widened_f32[:, :, :, :depth_planes])
    per_dir.append(pack_terms(0.5 * (forward - backward), eig_count))
    packed_dirs = [per_dir]
    slab = 0
    row_block = local_block[slab]
    row_block = row_block.reshape(eig_count, 2, 3, depth_planes, LXY, LXY).astype(jnp.float32)
    per_mom = []
    for mom_first in range(0, NMOM, 2):
        twisted = phase_twist(
            row_block, cosine_all[mom_first : mom_first + 2], sine_all[mom_first : mom_first + 2]
        )
        per_dir = []
        for dir_index in range(3):
            product = lax.dot_general(
                twisted,
                packed_dirs[slab][dir_index],
                (((1,), (1,)), ((), ())),
                preferred_element_type=jnp.float32,
            )
            per_dir.append(product.reshape(2, eig_count, 2 * eig_count))
        per_mom.append(jnp.stack(per_dir, axis=2))
    mom_block = jnp.concatenate(per_mom, axis=0)
    per_slab = [jnp.transpose(mom_block, (1, 0, 2, 3))]
    summed = lax.psum_scatter(jnp.stack(per_slab, axis=1), "space", scatter_dimension=0, tiled=True)
    dir_select = (directions[:, None] == jnp.arange(NDIR, dtype=jnp.int32)[None, :]).astype(
        jnp.float32
    )
    return jnp.einsum("dm,itpmq->itpdq", dir_select, summed, precision=lax.Precision.HIGHEST)


LANES = 128


def add_links(link, rows, field, sign):
    real, imag = [], []
    for a in range(3):
        re_sum = im_sum = None
        for b in range(3):
            row = rows + (3 * a + b if sign > 0 else 3 * b + a)
            link_re, link_im = link(row), link(row + 9)
            re_b, im_b = field[b], field[3 + b]
            if sign > 0:
                re_t = link_re * re_b - link_im * im_b
                im_t = link_re * im_b + link_im * re_b
            else:
                re_t = link_re * re_b + link_im * im_b
                im_t = link_re * im_b - link_im * re_b
            re_sum = re_t if re_sum is None else re_sum + re_t
            im_sum = im_t if im_sum is None else im_sum + im_t
        real.append(re_sum)
        imag.append(im_sum)
    return real + imag


def kernel(
    count, depth, groups, field_ref, links_ref, momenta_ref, directions_ref, out_ref,
    local, ahead, held, held_ahead, held_links, wide_links, tab_ref, twisted, packed, edge, sent, got, sums,
    pay_send, pay_recv, ahead_send, ahead_recv, link_send, link_recv, own_sem, part_send, part_recv,
):
    me = lax.axis_index("space")
    peers = lambda step: lax.rem(me + step, count)
    rows_of = field_ref.shape[3]
    eigs = count * rows_of
    moms = momenta_ref.shape[1]
    per_row = LANES // LXY
    pieces = depth // per_row
    main_k = 6 * depth * LANES

    own_field = pltpu.make_async_copy(field_ref, local, own_sem.at[2])
    own_field.start()
    barrier = pltpu.get_barrier_semaphore()
    for step in range(1, count):
        pl.semaphore_signal(barrier, inc=1, device_id={"space": peers(step)}, device_id_type=pl.DeviceIdType.MESH)
    pl.semaphore_wait(barrier, count - 1)

    def link_copy(target, source):
        return pltpu.make_async_remote_copy(
            src_ref=links_ref.at[:, :, pl.ds(pl.multiple_of(target * LANES, LANES), LANES)],
            dst_ref=held_links.at[source],
            send_sem=link_send.at[target], recv_sem=link_recv.at[source],
            device_id={"space": target}, device_id_type=pl.DeviceIdType.MESH,
        )

    def pay_copy(target, source):
        return pltpu.make_async_remote_copy(
            src_ref=field_ref.at[:, :, target], dst_ref=held.at[source],
            send_sem=pay_send.at[target], recv_sem=pay_recv.at[source],
            device_id={"space": target}, device_id_type=pl.DeviceIdType.MESH,
        )

    def ahead_copy(target, source):
        return pltpu.make_async_remote_copy(
            src_ref=ahead.at[target], dst_ref=held_ahead.at[source],
            send_sem=ahead_send.at[target], recv_sem=ahead_recv.at[source],
            device_id={"space": target}, device_id_type=pl.DeviceIdType.MESH,
        )

    def part_copy(group, target, source):
        span = pl.ds(group * (moms // groups), moms // groups)
        return pltpu.make_async_remote_copy(
            src_ref=sent.at[target, span], dst_ref=got.at[source, span],
            send_sem=part_send.at[group, target], recv_sem=part_recv.at[group, source],
            device_id={"space": target}, device_id_type=pl.DeviceIdType.MESH,
        )

    own_pay = pltpu.make_async_copy(field_ref.at[:, :, me], held.at[me], own_sem.at[0])
    own_links = pltpu.make_async_copy(
        links_ref.at[:, :, pl.ds(pl.multiple_of(me * LANES, LANES), LANES)], held_links.at[me], own_sem.at[1]
    )
    own_pay.start()
    own_links.start()
    for step in range(1, count):
        link_copy(peers(step), me).start()
    half = lax.rem(me, 2)
    high = me // 2
    tall = count // 2
    order = [0] + [d if s == 0 else tall - d for d in range(1, (tall + 1) // 2) for s in (0, 1)]
    if tall % 2 == 0:
        order.append(tall // 2)
    column = lambda hop: lax.rem(high + hop, tall)
    for hop in order:
        for side in (1, 0):
            if hop == 0 and side == 0:
                continue
            pay_copy(2 * column(hop) + lax.rem(half + side, 2), me).start()

    roll = lambda value, shift: pltpu.roll(value, shift % LANES, 1)
    lane_row = lax.broadcasted_iota(jnp.int32, (rows_of, LANES), 1) // LXY
    own_field.wait()

    def gather_ahead(target, carry):
        block = lax.rem(target + 1, count)
        for c in range(6):
            for m in range(pieces):
                line = local[c, m * per_row, block].astype(jnp.float32)
                for q in range(1, per_row):
                    value = local[c, m * per_row + q, block].astype(jnp.float32)
                    line = jnp.where(lane_row == q, roll(value, LXY * q), line)
                ahead[target, c, m] = line.astype(jnp.bfloat16)
        return carry

    lax.fori_loop(0, count, gather_ahead, 0)
    for hop in order:
        for side in (1, 0):
            if hop == 0 and side == 0:
                continue
            ahead_copy(2 * column(hop) + lax.rem(half + side, 2), me).start()
    held_ahead[me] = ahead[me]

    mom_row = lax.broadcasted_iota(jnp.int32, (moms, LANES), 0)
    mom_lane = lax.broadcasted_iota(jnp.int32, (moms, LANES), 1)
    moved = []
    for axis in range(3):
        values = jnp.zeros((moms, LANES), jnp.int32)
        for p in range(moms):
            values = jnp.where(mom_row == p, momenta_ref[axis, p], values)
        moved.append(values)
    part_x = ((moved[0] * (mom_lane % LXY)) & (LXY - 1)).astype(jnp.float32) / LXY
    for place in range(depth + pieces):
        if place < depth:
            y_at, z_at = me * per_row + mom_lane // LXY, place
        else:
            y_at, z_at = (me + 1) * per_row, (place - depth) * per_row + mom_lane // LXY
        fraction = part_x + ((moved[1] * y_at) & (LXY - 1)).astype(jnp.float32) / LXY
        fraction = fraction + ((moved[2] * z_at) & (depth - 1)).astype(jnp.float32) / depth
        tab_ref[place, 0:moms] = jnp.cos(TWO_PI * fraction)
        tab_ref[place, moms:] = jnp.sin(TWO_PI * fraction)

    own_links.wait()
    for step in range(1, count):
        link_copy(peers(step), peers(step)).wait_recv()
    wide_links[...] = held_links[...].astype(jnp.float32)
    own_pay.wait()

    lane = lax.broadcasted_iota(jnp.int32, (2 * rows_of, LANES), 1)
    x_of = lax.rem(lane, LXY)
    quarter = lane // LXY
    row_last = quarter == LANES // LXY - 1
    row_first = quarter == 0

    def next_x(value):
        return jnp.where(x_of == LXY - 1, roll(value, LXY - 1), roll(value, -1))

    def last_x(value):
        return jnp.where(x_of == 0, roll(value, 1 - LXY), roll(value, 1))

    def do_pair(pair):
        first = pl.multiple_of(pair * 2 * rows_of, 2 * rows_of)
        eig_span = pl.ds(first, 2 * rows_of)

        def load(c, place):
            return held[pl.ds(2 * pair, 2), c, place].astype(jnp.float32).reshape(2 * rows_of, LANES)

        def load_ahead(c, m):
            return held_ahead[pl.ds(2 * pair, 2), c, m].astype(jnp.float32).reshape(2 * rows_of, LANES)

        def store_packed(ref, base, values, offset):
            vals = [value.astype(jnp.bfloat16) for value in values]
            for c in range(6):
                span = pl.ds(pl.multiple_of(offset(c), LANES), LANES)
                ref[pl.ds(base + first, 2 * rows_of), span] = vals[c]
                swapped = vals[c + 3] if c < 3 else -vals[c - 3]
                ref[pl.ds(base + eigs + first, 2 * rows_of), span] = swapped

        def twist(field, place, offset):
            for p in range(moms):
                cosine = tab_ref[place, p][None]
                sine = tab_ref[place, moms + p][None]
                for c in range(3):
                    real = field[c] * cosine - field[c + 3] * sine
                    imag = field[c] * sine + field[c + 3] * cosine
                    for part, value in ((c, real), (c + 3, imag)):
                        span = pl.ds(pl.multiple_of(offset(part), LANES), LANES)
                        twisted[pl.ds(p * eigs + first, 2 * rows_of), span] = value.astype(jnp.bfloat16)

        def piece(m, carry):
            halo = [load_ahead(c, m) for c in range(6)]
            halo_k = lambda c: main_k + (c * pieces + m) * LANES
            twist(halo, depth + m, halo_k)
            tails = [None] * 6
            for q in range(4):
                z = m * 4 + q
                z_up, z_down = lax.rem(z + 1, depth), lax.rem(z + depth - 1, depth)
                main = lambda c: (c * depth + z) * LANES
                at = lambda where: lambda row: wide_links[where, row // 18, row % 18][None]
                field = [load(c, z) for c in range(6)]
                twist(field, z, main)
                forward = add_links(at(z), 0, [next_x(v) for v in field], 1)
                backward = [last_x(v) for v in add_links(at(z), 0, field, -1)]
                store_packed(packed, 0, [0.5 * (f - b) for f, b in zip(forward, backward)], main)
                shifted = [
                    jnp.where(row_last, roll(h, LANES - LXY - LXY * q), roll(v, -LXY))
                    for v, h in zip(field, halo)
                ]
                forward = add_links(at(z), 18, shifted, 1)
                behind = add_links(at(z), 18, field, -1)
                store_packed(
                    packed, 2 * eigs,
                    [0.5 * (f - jnp.where(row_first, 0.0, roll(b, LXY))) for f, b in zip(forward, behind)],
                    main,
                )
                for c in range(6):
                    tail = -0.5 * roll(behind[c], LXY * (q + 1))
                    tails[c] = tail if q == 0 else jnp.where(quarter == q, tail, tails[c])
                forward = add_links(at(z), 36, [load(c, z_up) for c in range(6)], 1)
                backward = add_links(at(z_down), 36, [load(c, z_down) for c in range(6)], -1)
                store_packed(packed, 4 * eigs, [0.5 * (f - b) for f, b in zip(forward, backward)], main)
            store_packed(edge, 0, tails, lambda c: (c * pieces + m) * LANES)
            return carry

        lax.fori_loop(0, pieces, piece, 0)

    for hop in order:
        pair = column(hop)
        for side in (1, 0):
            if hop == 0 and side == 0:
                continue
            source = 2 * pair + lax.rem(half + side, 2)
            pay_copy(source, source).wait_recv()
            ahead_copy(source, source).wait_recv()
        do_pair(pair)

    each = moms // groups
    contract = (((1,), (1,)), ((), ()))
    for group in range(groups):
        rows = pl.ds(group * each * eigs, each * eigs)
        product = lax.dot_general(
            twisted[rows, 0:main_k], packed[...], contract, preferred_element_type=jnp.float32
        )
        extra = lax.dot_general(
            twisted[rows, main_k:], edge[...], contract, preferred_element_type=jnp.float32
        )
        width = 2 * eigs
        for d in range(NDIR):
            block = product[:, d * width : (d + 1) * width]
            if d == 1:
                block = block + extra
            block = block.astype(jnp.float32).reshape(each, count, rows_of, width)
            for p in range(each):
                for target in range(count):
                    sent[target, group * each + p, d] = block[p, target].astype(jnp.bfloat16)
        for step in range(1, count):
            part_copy(group, peers(step), me).start()

    got[me] = sent[me]
    for group in range(groups):
        for step in range(1, count):
            part_copy(group, peers(step), peers(step)).wait_recv()
        for p in range(group * each, (group + 1) * each):
            for d in range(NDIR):
                total = got[0, p, d].astype(jnp.float32)
                for source in range(1, count):
                    total = total + got[source, p, d].astype(jnp.float32)
                sums[d, p] = total
    for d in range(NDIR):
        for p in range(moms):
            out_ref[:, d, p] = sums[directions_ref[d], p]

    for step in range(1, count):
        target = peers(step)
        link_copy(target, me).wait_send()
        pay_copy(target, me).wait_send()
        ahead_copy(target, me).wait_send()
        for group in range(groups):
            part_copy(group, target, me).wait_send()


def shards_by_rows(vectors, gauge_links, momenta, directions):
    count = lax.axis_size("space")
    eig_local = vectors.shape[1]
    eigs = eig_local * count
    moms = momenta.shape[0]
    depth = vectors.shape[3] // (LXY * LXY)
    pieces = depth * LXY // LANES
    field = jnp.transpose(vectors[0].reshape(eig_local, 6, depth, count, LANES), (1, 2, 3, 0, 4))

    groups = 2
    main_k = 6 * depth * LANES
    edge_k = 6 * pieces * LANES
    vmem = pl.BlockSpec(memory_space=pltpu.VMEM)
    part = (count, moms, NDIR, eig_local, 2 * eigs)
    summed = pl.pallas_call(
        lambda *refs: kernel(count, depth, groups, *refs),
        out_shape=jax.ShapeDtypeStruct((eig_local, NDIR, moms, 2 * eigs), jnp.float32),
        in_specs=[
            pl.BlockSpec(memory_space=pl.ANY),
            pl.BlockSpec(memory_space=pl.ANY),
            pl.BlockSpec(memory_space=pltpu.SMEM),
            pl.BlockSpec(memory_space=pltpu.SMEM),
        ],
        out_specs=vmem,
        scratch_shapes=[
            pltpu.VMEM(field.shape, jnp.bfloat16),
            pltpu.VMEM((count, 6, pieces, eig_local, LANES), jnp.bfloat16),
            pltpu.VMEM((count, 6, depth, eig_local, LANES), jnp.bfloat16),
            pltpu.VMEM((count, 6, pieces, eig_local, LANES), jnp.bfloat16),
            pltpu.VMEM((count, NDIR, 18, LANES), jnp.bfloat16),
            pltpu.VMEM((count, NDIR, 18, LANES), jnp.float32),
            pltpu.VMEM((depth + pieces, 2 * moms, LANES), jnp.float32),
            pltpu.VMEM((moms * eigs, main_k + edge_k), jnp.bfloat16),
            pltpu.VMEM((NDIR * 2 * eigs, main_k), jnp.bfloat16),
            pltpu.VMEM((2 * eigs, edge_k), jnp.bfloat16),
            pltpu.VMEM(part, jnp.bfloat16),
            pltpu.VMEM(part, jnp.bfloat16),
            pltpu.VMEM((NDIR, moms, eig_local, 2 * eigs), jnp.float32),
            pltpu.SemaphoreType.DMA((count,)),
            pltpu.SemaphoreType.DMA((count,)),
            pltpu.SemaphoreType.DMA((count,)),
            pltpu.SemaphoreType.DMA((count,)),
            pltpu.SemaphoreType.DMA((count,)),
            pltpu.SemaphoreType.DMA((count,)),
            pltpu.SemaphoreType.DMA((3,)),
            pltpu.SemaphoreType.DMA((groups, count)),
            pltpu.SemaphoreType.DMA((groups, count)),
        ],
        compiler_params=pltpu.CompilerParams(collective_id=0, has_side_effects=True),
        name="elementals",
    )(field, gauge_links[0], momenta.T, directions)
    return jnp.transpose(summed, (0, 2, 1, 3))[:, None]


def shards(vectors, gauge_links, momenta, directions):
    count = lax.axis_size("space")
    depth = vectors.shape[3] // (LXY * LXY)
    by_rows = (
        vectors.shape[0] == 1
        and count * LANES == LXY * LXY
        and depth == count
        and depth & (depth - 1) == 0
        and vectors.shape[1] % 8 == 0
    )
    body = shards_by_rows if by_rows else shards_by_plane
    return body(vectors, gauge_links, momenta, directions)


def solution(mesh):
    return jax.shard_map(
        shards,
        mesh=mesh,
        in_specs=(
            P(("cfg", "tm"), "space", None, None),
            P(("cfg", "tm"), None, None, "space"),
            P(),
            P(),
        ),
        out_specs=P("space", ("cfg", "tm"), None, None, None),
        check_vma=False,
    )
```

profile of v0, /device:TPU:0, one launch (start us, length us, event | category | flops | bytes accessed | tf_op | source)
XLA Modules:
  0.0 49.6 jit_solution(13350786449001480039)
XLA Ops:
  0.0 48.0 %elementals.1 = f32[8,3,8,128]{3,2,1,0:T(8,128)} custom-call(bf16[6,8,8,8,128]{4,3,2,1,0:T(8,128)(2,1)} %bitcast.10, bf16[3,18,1024]{2,1,0:T(8,128)(2,1)} %bitcast.12, s32[3,8]{1,0:T(4,128)} %bitcast.13, s32[3]{0:T(128)} %refs_3_.1), custom_call_target="tpu_custom_call" | custom-call | tf_op jit(solution)/shard_map/elementals/pallas_call | solution.py:458
  48.0 1.5 %copy.7 = f32[8,1,8,3,128]{4,2,3,1,0:T(8,128)} copy(f32[8,1,8,3,128]{4,2,3,1,0:T(8,128)} %bitcast.11) | data formatting | bytes 196608
where the time goes:
time: 49.8 us; the launch traced here: 49.6 us
  Pallas kernels  48 us (96%)
  local copies, waits for them, and re-layouts  1.54 us (3%)
    pallas_call x1, Pallas kernels, shards_by_rows(): pl.pallas_call(lambda *refs: kernel(count, depth, groups, *refs), out_sha...  48 us
    unnamed x1, local copies, waits for them, and re-layouts  1.54 us

commit v1 on v0

v1 whole, which is shorter than its diff:
```python
import math

import jax
import jax.numpy as jnp
from jax import lax
from jax.experimental import pallas as pl
from jax.experimental.pallas import tpu as pltpu
from jax.sharding import PartitionSpec as P

LXY = 32
NMOM = 8
NDIR = 3


TWO_PI = 2.0 * math.pi


def with_halo(cells, sides, width):
    for axis, dim in sides:
        count = lax.axis_size(axis)
        head = lax.slice_in_dim(cells, 0, width, axis=dim)
        tail = lax.slice_in_dim(cells, cells.shape[dim] - width, cells.shape[dim], axis=dim)
        cells = jnp.concatenate(
            [
                lax.ppermute(tail, axis, [(i, (i + 1) % count) for i in range(count)]),
                cells,
                lax.ppermute(head, axis, [((i + 1) % count, i) for i in range(count)]),
            ],
            axis=dim,
        )
    return cells


def from_behind(block, axis, distance):
    devices = range(lax.axis_size(axis))
    route = [((i - distance) % len(devices), i) for i in devices]
    return lax.ppermute(block, axis, route)


def apply_link(link, field_f32):
    real_rows = []
    imag_rows = []
    for row_a in range(3):
        link_re = link[0, row_a, 0][None]
        link_im = link[1, row_a, 0][None]
        real_acc = link_re * field_f32[:, 0, 0] - link_im * field_f32[:, 1, 0]
        imag_acc = link_re * field_f32[:, 1, 0] + link_im * field_f32[:, 0, 0]
        for col_b in range(1, 3):
            link_re = link[0, row_a, col_b][None]
            link_im = link[1, row_a, col_b][None]
            real_acc = (
                real_acc + link_re * field_f32[:, 0, col_b] - link_im * field_f32[:, 1, col_b]
            )
            imag_acc = (
                imag_acc + link_re * field_f32[:, 1, col_b] + link_im * field_f32[:, 0, col_b]
            )
        real_rows.append(real_acc)
        imag_rows.append(imag_acc)
    return jnp.stack([jnp.stack(real_rows, axis=1), jnp.stack(imag_rows, axis=1)], axis=1)


def adjoint(link):
    return jnp.stack([jnp.swapaxes(link[0], 0, 1), -jnp.swapaxes(link[1], 0, 1)])


def pack_terms(derivative, eig_count):
    rounded = derivative.astype(jnp.bfloat16)
    rounded_re = rounded[:, 0]
    rounded_im = rounded[:, 1]
    swapped = jnp.stack([rounded_im, -rounded_re], axis=1)
    return jnp.concatenate([rounded, swapped], axis=0).reshape(2 * eig_count, -1)


def phase_angles(momenta, z_offset, depth_planes, z_length):
    z_coord = z_offset + jnp.arange(depth_planes, dtype=jnp.int32)
    y_coord = jnp.arange(LXY, dtype=jnp.int32)
    x_coord = jnp.arange(LXY, dtype=jnp.int32)
    mom_x = momenta[:, 0][:, None, None, None]
    mom_y = momenta[:, 1][:, None, None, None]
    mom_z = momenta[:, 2][:, None, None, None]
    fraction = (mom_x * x_coord[None, None, None, :] % LXY).astype(jnp.float32) / LXY
    fraction = fraction + (mom_y * y_coord[None, None, :, None] % LXY).astype(jnp.float32) / LXY
    fraction = (
        fraction + (mom_z * z_coord[None, :, None, None] % z_length).astype(jnp.float32) / z_length
    )
    return TWO_PI * fraction


def phase_twist(row_block, cosine_table, sine_table):
    vec_re = row_block[:, 0][None]
    vec_im = row_block[:, 1][None]
    cos_b = cosine_table[:, None, None]
    sin_b = sine_table[:, None, None]
    real_part = vec_re * cos_b - vec_im * sin_b
    imag_part = vec_re * sin_b + vec_im * cos_b
    twisted = jnp.stack([real_part, imag_part], axis=2).astype(jnp.bfloat16)
    return twisted.reshape(cosine_table.shape[0] * row_block.shape[0], -1)


def shards_by_plane(vectors, gauge_links, momenta, directions):
    space_count = lax.axis_size("space")
    slab_count = vectors.shape[0]
    eig_local = vectors.shape[1]
    eig_count = eig_local * space_count
    plane_size = LXY * LXY
    depth_planes = gauge_links.shape[3] // plane_size
    blocks = vectors.reshape(slab_count, eig_local, 6, space_count, depth_planes, plane_size)
    regrouped = lax.all_to_all(blocks, "space", split_axis=3, concat_axis=1, tiled=True)
    local_block = regrouped.reshape(slab_count, eig_count, 6, depth_planes, plane_size)
    extended = with_halo(local_block, (("space", 3),), 1)
    z_links = gauge_links[:, 2].reshape(slab_count, 18, depth_planes, plane_size)
    link_below = from_behind(z_links[:, :, depth_planes - 1, :], "space", 1)
    links_below = jnp.concatenate(
        [link_below[:, :, None, :], z_links[:, :, : depth_planes - 1, :]], axis=2
    )
    z_offset = lax.axis_index("space") * depth_planes
    angles = phase_angles(momenta, z_offset, depth_planes, depth_planes * space_count)
    cosine_all = jnp.cos(angles)
    sine_all = jnp.sin(angles)
    slab = 0
    field_f32 = (
        local_block[slab].reshape(eig_count, 2, 3, depth_planes, LXY, LXY).astype(jnp.float32)
    )
    widened_f32 = (
        extended[slab].reshape(eig_count, 2, 3, depth_planes + 2, LXY, LXY).astype(jnp.float32)
    )
    slab_links = gauge_links[slab].reshape(3, 2, 3, 3, depth_planes, LXY, LXY).astype(jnp.float32)
    prev_links = links_below[slab].reshape(2, 3, 3, depth_planes, LXY, LXY).astype(jnp.float32)
    per_dir = []
    for dir_index, roll_axis in ((0, -1), (1, -2)):
        forward = apply_link(slab_links[dir_index], jnp.roll(field_f32, -1, axis=roll_axis))
        backward = jnp.roll(
            apply_link(adjoint(slab_links[dir_index]), field_f32), 1, axis=roll_axis
        )
        per_dir.append(pack_terms(0.5 * (forward - backward), eig_count))
    forward = apply_link(slab_links[2], widened_f32[:, :, :, 2:])
    backward = apply_link(adjoint(prev_links), widened_f32[:, :, :, :depth_planes])
    per_dir.append(pack_terms(0.5 * (forward - backward), eig_count))
    packed_dirs = [per_dir]
    slab = 0
    row_block = local_block[slab]
    row_block = row_block.reshape(eig_count, 2, 3, depth_planes, LXY, LXY).astype(jnp.float32)
    per_mom = []
    for mom_first in range(0, NMOM, 2):
        twisted = phase_twist(
            row_block, cosine_all[mom_first : mom_first + 2], sine_all[mom_first : mom_first + 2]
        )
        per_dir = []
        for dir_index in range(3):
            product = lax.dot_general(
                twisted,
                packed_dirs[slab][dir_index],
                (((1,), (1,)), ((), ())),
                preferred_element_type=jnp.float32,
            )
            per_dir.append(product.reshape(2, eig_count, 2 * eig_count))
        per_mom.append(jnp.stack(per_dir, axis=2))
    mom_block = jnp.concatenate(per_mom, axis=0)
    per_slab = [jnp.transpose(mom_block, (1, 0, 2, 3))]
    summed = lax.psum_scatter(jnp.stack(per_slab, axis=1), "space", scatter_dimension=0, tiled=True)
    dir_select = (directions[:, None] == jnp.arange(NDIR, dtype=jnp.int32)[None, :]).astype(
        jnp.float32
    )
    return jnp.einsum("dm,itpmq->itpdq", dir_select, summed, precision=lax.Precision.HIGHEST)


LANES = 128


def add_links(link, rows, field, sign):
    real, imag = [], []
    for a in range(3):
        re_sum = im_sum = None
        for b in range(3):
            row = rows + (3 * a + b if sign > 0 else 3 * b + a)
            link_re, link_im = link(row), link(row + 9)
            re_b, im_b = field[b], field[3 + b]
            if sign > 0:
                re_t = link_re * re_b - link_im * im_b
                im_t = link_re * im_b + link_im * re_b
            else:
                re_t = link_re * re_b + link_im * im_b
                im_t = link_re * im_b - link_im * re_b
            re_sum = re_t if re_sum is None else re_sum + re_t
            im_sum = im_t if im_sum is None else im_sum + im_t
        real.append(re_sum)
        imag.append(im_sum)
    return real + imag


def spread(tiles, lane_group, roll):
    first = []
    for a, b in ((0, 1), (2, 3)):
        even = lane_group % 2 == 0
        first.append(jnp.where(even, tiles[a], roll(tiles[b], LXY)))
        first.append(jnp.where(even, roll(tiles[a], -LXY), tiles[b]))
    low = lane_group < 2
    out = [None] * 4
    for bit in range(2):
        near, far = first[bit], first[2 + bit]
        out[bit] = jnp.where(low, near, roll(far, 2 * LXY))
        out[2 + bit] = jnp.where(low, roll(near, -2 * LXY), far)
    return out


def kernel(
    count, depth, groups, field_ref, links_ref, momenta_ref, directions_ref, out_ref,
    local, stage, held, halo, held_links, wide_links, tab_ref, twisted, packed, packed_y, acc, acc_y, sent, got, sums,
    pay_send, pay_recv, halo_send, halo_recv, pass_send, pass_recv, link_send, link_recv, own_sem, part_send, part_recv,
):
    me = lax.axis_index("space")
    peers = lambda step: lax.rem(me + step, count)
    rows_of = field_ref.shape[3]
    eigs = count * rows_of
    moms = momenta_ref.shape[1]
    per_row = LANES // LXY
    pieces = depth // per_row
    row_k = 6 * pieces * LANES
    tall = count // 2
    half = lax.rem(me, 2)
    high = me // 2
    place_of = lambda device: lax.rem(device, 2) * (count - 1 - 2 * (device // 2)) + device // 2
    block = place_of(me)
    crossings = (tall // 2 - 1, tall + tall // 2 - 1)
    device_at = lambda place: 2 * place if place < tall else 2 * (count - 1 - place) + 1
    remote = lambda **rest: pltpu.make_async_remote_copy(device_id_type=pl.DeviceIdType.MESH, **rest)

    own_field = pltpu.make_async_copy(field_ref, local, own_sem.at[0])
    own_field.start()
    barrier = pltpu.get_barrier_semaphore()
    for step in range(1, count):
        pl.semaphore_signal(barrier, inc=1, device_id={"space": peers(step)}, device_id_type=pl.DeviceIdType.MESH)
    own_links = pltpu.make_async_copy(
        links_ref.at[:, :, pl.ds(pl.multiple_of(block * LANES, LANES), LANES)], held_links.at[me], own_sem.at[1]
    )
    own_links.start()

    def link_copy(target, source):
        return remote(
            src_ref=links_ref.at[:, :, pl.ds(pl.multiple_of(place_of(target) * LANES, LANES), LANES)],
            dst_ref=held_links.at[source],
            send_sem=link_send.at[target], recv_sem=link_recv.at[source], device_id={"space": target},
        )

    def pay_copy(row, target, source):
        return remote(
            src_ref=stage.at[place_of(target), row], dst_ref=held.at[row, source],
            send_sem=pay_send.at[row, target], recv_sem=pay_recv.at[row, source], device_id={"space": target},
        )

    def halo_copy(cross, source):
        place = crossings[cross]
        return remote(
            src_ref=stage.at[(place + 1) % count, 0], dst_ref=halo.at[source],
            send_sem=halo_send.at[cross], recv_sem=halo_recv.at[source], device_id={"space": device_at(place)},
        )

    def pass_copy():
        behind = lax.rem(block + count - 1, count)
        back = jnp.where(behind < tall, 2 * behind, 2 * (count - 1 - behind) + 1)
        return remote(
            src_ref=held.at[0], dst_ref=halo, send_sem=pass_send.at[0], recv_sem=pass_recv.at[0],
            device_id={"space": back},
        )

    def part_copy(group, target, source):
        span = pl.ds(group * (moms // groups), moms // groups)
        return remote(
            src_ref=sent.at[target, span], dst_ref=got.at[source, span],
            send_sem=part_send.at[group, target], recv_sem=part_recv.at[group, source], device_id={"space": target},
        )

    at_crossing = (block == crossings[0]) | (block == crossings[1])
    after_crossing = (block == crossings[0] + 1) | (block == (crossings[1] + 1) % count)
    roll = lambda value, shift: pltpu.roll(value, shift % LANES, 1)
    group_of = lambda rows: lax.broadcasted_iota(jnp.int32, (rows, LANES), 1) // LXY
    own_field.wait()

    def arrange(target, carry):
        lanes = group_of(rows_of)
        for c in range(6):
            for m in range(pieces):
                tiles = [local[c, m * per_row + q, target].astype(jnp.float32) for q in range(per_row)]
                for r, tile in enumerate(spread(tiles, lanes, roll)):
                    stage[target, r, c, m] = tile.astype(jnp.bfloat16)
        return carry

    lax.fori_loop(0, count, arrange, 0)
    pl.semaphore_wait(barrier, count - 1)

    for step in range(1, count):
        link_copy(peers(step), me).start()
    order = [0] + [d if s == 0 else tall - d for d in range(1, (tall + 1) // 2) for s in (0, 1)]
    if tall % 2 == 0:
        order.append(tall // 2)
    column = lambda hop: lax.rem(high + hop, tall)
    beside = [(hop, side) for hop in order for side in (1, 0)][:]
    beside.remove((0, 0))
    for row in range(per_row):
        for hop, side in beside:
            pay_copy(row, 2 * column(hop) + lax.rem(half + side, 2), me).start()
        if row == 1:
            for cross, place in enumerate(crossings):
                @pl.when(me != device_at(place))
                def _():
                    halo_copy(cross, me).start()
    for row in range(per_row):
        held[row, me] = stage[block, row]

    @pl.when(at_crossing)
    def _():
        halo[me] = stage[lax.rem(block + 1, count), 0]

    mom_row = lax.broadcasted_iota(jnp.int32, (moms, LANES), 0)
    mom_lane = lax.broadcasted_iota(jnp.int32, (moms, LANES), 1)
    moved = []
    for axis in range(3):
        values = jnp.zeros((moms, LANES), jnp.int32)
        for p in range(moms):
            values = jnp.where(mom_row == p, momenta_ref[axis, p], values)
        moved.append(values)
    part_x = ((moved[0] * (mom_lane % LXY)) & (LXY - 1)).astype(jnp.float32) / LXY
    for row in range(per_row + 1):
        for m in range(pieces):
            y_at = block * per_row + row
            z_at = m * per_row + mom_lane // LXY
            fraction = part_x + ((moved[1] * y_at) & (LXY - 1)).astype(jnp.float32) / LXY
            fraction = fraction + ((moved[2] * z_at) & (depth - 1)).astype(jnp.float32) / depth
            tab_ref[row * pieces + m, 0:moms] = jnp.cos(TWO_PI * fraction)
            tab_ref[row * pieces + m, moms:] = jnp.sin(TWO_PI * fraction)

    own_links.wait()
    for step in range(1, count):
        link_copy(peers(step), peers(step)).wait_recv()
    for m in range(pieces):
        for mu in range(NDIR):
            tiles = [held_links[m * per_row + q, mu].astype(jnp.float32) for q in range(per_row)]
            for r, tile in enumerate(spread(tiles, group_of(tiles[0].shape[0]), roll)):
                wide_links[r, m, mu] = 0.5 * tile

    wide = 2 * rows_of
    x_of = lax.rem(lax.broadcasted_iota(jnp.int32, (wide, LANES), 1), LXY)
    quarter = group_of(wide)

    def next_x(value):
        return jnp.where(x_of == LXY - 1, roll(value, LXY - 1), roll(value, -1))

    def last_x(value):
        return jnp.where(x_of == 0, roll(value, 1 - LXY), roll(value, 1))

    def links_at(row, m):
        return lambda entry: wide_links[row, m, entry // 18, entry % 18][None]

    def load_from(ref, pair, row, m):
        if row is None:
            return [ref[pl.ds(2 * pair, 2), c, m].astype(jnp.float32).reshape(wide, LANES) for c in range(6)]
        return [ref[row, pl.ds(2 * pair, 2), c, m].astype(jnp.float32).reshape(wide, LANES) for c in range(6)]

    def store_packed(ref, base, first, values, row, m):
        vals = [value.astype(jnp.bfloat16) for value in values]
        for c in range(6):
            span = pl.ds(row * row_k + (c * pieces + m) * LANES, LANES)
            ref[pl.ds(base + first, wide), span] = vals[c]
            ref[pl.ds(base + eigs + first, wide), span] = vals[c + 3] if c < 3 else -vals[c - 3]

    def twist(field, first, row, m):
        for p in range(moms):
            cosine = tab_ref[row * pieces + m, p][None]
            sine = tab_ref[row * pieces + m, moms + p][None]
            for c in range(3):
                real = field[c] * cosine - field[c + 3] * sine
                imag = field[c] * sine + field[c + 3] * cosine
                for part, value in ((c, real), (c + 3, imag)):
                    span = pl.ds(row * row_k + (part * pieces + m) * LANES, LANES)
                    twisted[pl.ds(p * eigs + first, wide), span] = value.astype(jnp.bfloat16)

    def along_y(pair, first, row, m):
        ahead = load_from(held, pair, row + 1, m) if row + 1 < per_row else load_from(halo, pair, None, m)
        values = add_links(links_at(row, m), 18, ahead, 1)
        if row:
            behind = add_links(links_at(row - 1, m), 18, load_from(held, pair, row - 1, m), -1)
            values = [f - b for f, b in zip(values, behind)]
        store_packed(packed_y, 0, first, values, row, m)

    def do_row(row, pair):
        first = pl.multiple_of(pair * wide, wide)
        behind = []
        for m in range(pieces):
            field = load_from(held, pair, row, m)
            twist(field, first, row, m)
            forward = add_links(links_at(row, m), 0, [next_x(v) for v in field], 1)
            backward = [last_x(v) for v in add_links(links_at(row, m), 0, field, -1)]
            store_packed(packed, 0, first, [f - b for f, b in zip(forward, backward)], row, m)
        for m in range(pieces):
            behind.append([roll(v, LXY) for v in add_links(links_at(row, m), 36, load_from(held, pair, row, m), -1)])
        for m in range(pieces):
            field, after = load_from(held, pair, row, m), load_from(held, pair, row, (m + 1) % pieces)
            shifted = [
                jnp.where(quarter == per_row - 1, roll(a, -LXY), roll(v, -LXY)) for v, a in zip(field, after)
            ]
            forward = add_links(links_at(row, m), 36, shifted, 1)
            backward = [
                jnp.where(quarter == 0, a, b) for a, b in zip(behind[(m - 1) % pieces], behind[m])
            ]
            store_packed(packed, 2 * eigs, first, [f - b for f, b in zip(forward, backward)], row, m)
        if row:
            for m in range(pieces):
                along_y(pair, first, row - 1, m)
        if row == per_row - 1:
            for m in range(pieces):
                along_y(pair, first, row, m)
                tails = add_links(links_at(row, m), 18, load_from(held, pair, row, m), -1)
                store_packed(packed_y, 0, first, [-v for v in tails], row + 1, m)

    contract = (((1,), (1,)), ((), ()))

    def dot_of(rows, ref, first_row, last_row):
        span = slice(first_row * row_k, last_row * row_k)
        return lax.dot_general(twisted[rows, span], ref[:, span], contract, preferred_element_type=jnp.float32)

    every = slice(0, moms * eigs)
    for row in range(per_row):
        def one(i, carry):
            pair = column(jnp.where(i < 2, i, tall + 1 - i))
            for side in range(2):
                source = 2 * pair + side

                @pl.when(source != me)
                def _():
                    pay_copy(row, source, source).wait_recv()
            do_row(row, pair)
            return carry

        if row == per_row - 1:
            @pl.when(at_crossing)
            def _():
                for step in range(1, count):
                    halo_copy(0, peers(step)).wait_recv()

            @pl.when(jnp.logical_not(at_crossing))
            def _():
                pass_copy().wait_recv()

            def last(pair, carry):
                for m in range(pieces):
                    twist(load_from(halo, pair, None, m), pl.multiple_of(pair * wide, wide), per_row, m)
                return carry

            lax.fori_loop(0, tall, last, 0)
        lax.fori_loop(0, tall, one, 0)
        if row == 0:
            @pl.when(jnp.logical_not(after_crossing))
            def _():
                pass_copy().start()
        if row == 1:
            acc[...] = dot_of(every, packed, 0, 2)
        if row == 2:
            acc[...] += dot_of(every, packed, 2, 3)
            acc_y[...] = dot_of(every, packed_y, 0, 2)

    each = moms // groups
    width = 2 * eigs
    for group in range(groups):
        rows = slice(group * each * eigs, (group + 1) * each * eigs)
        along = acc[rows] + dot_of(rows, packed, per_row - 1, per_row)
        across = acc_y[rows] + dot_of(rows, packed_y, 2, per_row + 1)
        for d, result in enumerate((along[:, :width], across, along[:, width:])):
            result = result.reshape(each, count, rows_of, width)
            for p in range(each):
                for target in range(count):
                    sent[target, group * each + p, d] = result[p, target].astype(jnp.bfloat16)
        for step in range(1, count):
            part_copy(group, peers(step), me).start()

    got[me] = sent[me]
    for group in range(groups):
        for step in range(1, count):
            part_copy(group, peers(step), peers(step)).wait_recv()
        for p in range(group * each, (group + 1) * each):
            for d in range(NDIR):
                total = got[0, p, d].astype(jnp.float32)
                for source in range(1, count):
                    total = total + got[source, p, d].astype(jnp.float32)
                sums[d, p] = total
    for d in range(NDIR):
        for p in range(moms):
            out_ref[:, d, p] = sums[directions_ref[d], p]

    for step in range(1, count):
        target = peers(step)
        link_copy(target, me).wait_send()
        for row in range(per_row):
            pay_copy(row, target, me).wait_send()
        for group in range(groups):
            part_copy(group, target, me).wait_send()
    for cross, place in enumerate(crossings):
        @pl.when(me != device_at(place))
        def _():
            halo_copy(cross, me).wait_send()

    @pl.when(jnp.logical_not(after_crossing))
    def _():
        pass_copy().wait_send()


def shards_by_rows(vectors, gauge_links, momenta, directions):
    count = lax.axis_size("space")
    eig_local = vectors.shape[1]
    eigs = eig_local * count
    moms = momenta.shape[0]
    depth = vectors.shape[3] // (LXY * LXY)
    per_row = LANES // LXY
    pieces = depth // per_row
    field = jnp.transpose(vectors[0].reshape(eig_local, 6, depth, count, LANES), (1, 2, 3, 0, 4))

    groups = 2
    row_k = 6 * pieces * LANES
    vmem = pl.BlockSpec(memory_space=pltpu.VMEM)
    part = (count, moms, NDIR, eig_local, 2 * eigs)
    lump = (6, pieces, eig_local, LANES)
    summed = pl.pallas_call(
        lambda *refs: kernel(count, depth, groups, *refs),
        out_shape=jax.ShapeDtypeStruct((eig_local, NDIR, moms, 2 * eigs), jnp.float32),
        in_specs=[
            pl.BlockSpec(memory_space=pl.ANY),
            pl.BlockSpec(memory_space=pl.ANY),
            pl.BlockSpec(memory_space=pltpu.SMEM),
            pl.BlockSpec(memory_space=pltpu.SMEM),
        ],
        out_specs=vmem,
        scratch_shapes=[
            pltpu.VMEM(field.shape, jnp.bfloat16),
            pltpu.VMEM((count, per_row) + lump, jnp.bfloat16),
            pltpu.VMEM((per_row, count) + lump, jnp.bfloat16),
            pltpu.VMEM((count,) + lump, jnp.bfloat16),
            pltpu.VMEM((count, NDIR, 18, LANES), jnp.bfloat16),
            pltpu.VMEM((per_row, pieces, NDIR, 18, LANES), jnp.float32),
            pltpu.VMEM(((per_row + 1) * pieces, 2 * moms, LANES), jnp.float32),
            pltpu.VMEM((moms * eigs, (per_row + 1) * row_k), jnp.bfloat16),
            pltpu.VMEM((4 * eigs, per_row * row_k), jnp.bfloat16),
            pltpu.VMEM((2 * eigs, (per_row + 1) * row_k), jnp.bfloat16),
            pltpu.VMEM((moms * eigs, 4 * eigs), jnp.float32),
            pltpu.VMEM((moms * eigs, 2 * eigs), jnp.float32),
            pltpu.VMEM(part, jnp.bfloat16),
            pltpu.VMEM(part, jnp.bfloat16),
            pltpu.VMEM((NDIR, moms, eig_local, 2 * eigs), jnp.float32),
            pltpu.SemaphoreType.DMA((per_row, count)),
            pltpu.SemaphoreType.DMA((per_row, count)),
            pltpu.SemaphoreType.DMA((2,)),
            pltpu.SemaphoreType.DMA((count,)),
            pltpu.SemaphoreType.DMA((1,)),
            pltpu.SemaphoreType.DMA((1,)),
            pltpu.SemaphoreType.DMA((count,)),
            pltpu.SemaphoreType.DMA((count,)),
            pltpu.SemaphoreType.DMA((2,)),
            pltpu.SemaphoreType.DMA((groups, count)),
            pltpu.SemaphoreType.DMA((groups, count)),
        ],
        compiler_params=pltpu.CompilerParams(collective_id=0, has_side_effects=True),
        name="elementals",
    )(field, gauge_links[0], momenta.T, directions)
    return jnp.transpose(summed, (0, 2, 1, 3))[:, None]


def shards(vectors, gauge_links, momenta, directions):
    count = lax.axis_size("space")
    depth = vectors.shape[3] // (LXY * LXY)
    by_rows = (
        vectors.shape[0] == 1
        and count * LANES == LXY * LXY
        and depth == count
        and depth & (depth - 1) == 0
        and depth == 2 * (LANES // LXY)
        and vectors.shape[1] % 8 == 0
    )
    body = shards_by_rows if by_rows else shards_by_plane
    return body(vectors, gauge_links, momenta, directions)


def solution(mesh):
    return jax.shard_map(
        shards,
        mesh=mesh,
        in_specs=(
            P(("cfg", "tm"), "space", None, None),
            P(("cfg", "tm"), None, None, "space"),
            P(),
            P(),
        ),
        out_specs=P("space", ("cfg", "tm"), None, None, None),
        check_vma=False,
    )
```

time: 49.8 us -> 45.7 us (0.918)
  Pallas kernels: 48 us -> 44 us
    pallas_call x1, Pallas kernels: 48 us -> 44 us  [shards_by_rows(): pl.pallas_call(lambda *refs: kernel(count, depth, groups, *refs), out_sha...]
where the time goes in v1:
time: 45.7 us; the launch traced here: 45.6 us
  Pallas kernels  44 us (96%)
  local copies, waits for them, and re-layouts  1.54 us (3%)
    pallas_call x1, Pallas kernels, shards_by_rows(): pl.pallas_call(lambda *refs: kernel(count, depth, groups, *refs), out_sha...  44 us
    unnamed x1, local copies, waits for them, and re-layouts  1.54 us

profile of v1, /device:TPU:0, one launch (start us, length us, event | category | flops | bytes accessed | tf_op | source)
XLA Modules:
  0.0 45.6 jit_solution(5753041011257342305)
XLA Ops:
  0.0 44.0 %elementals.1 = f32[8,3,8,128]{3,2,1,0:T(8,128)} custom-call(bf16[6,8,8,8,128]{4,3,2,1,0:T(8,128)(2,1)} %bitcast.10, bf16[3,18,1024]{2,1,0:T(8,128)(2,1)} %bitcast.12, s32[3,8]{1,0:T(4,128)} %bitcast.13, s32[3]{0:T(128)} %refs_3_.1), custom_call_target="tpu_custom_call" | custom-call | tf_op jit(solution)/shard_map/elementals/pallas_call | solution.py:521
  44.0 1.5 %copy.7 = f32[8,1,8,3,128]{4,2,3,1,0:T(8,128)} copy(f32[8,1,8,3,128]{4,2,3,1,0:T(8,128)} %bitcast.11) | data formatting | bytes 196608

commit v2 on v1

--- a/solution.py
+++ b/solution.py
@@ -205,7 +205,7 @@
 
 def kernel(
     count, depth, groups, field_ref, links_ref, momenta_ref, directions_ref, out_ref,
-    local, stage, held, halo, held_links, wide_links, tab_ref, twisted, packed, packed_y, acc, acc_y, sent, got, sums,
+    local, stage, held, halo, held_links, wide_links, tab_ref, twisted, packed, packed_y, acc, acc_y, sent, got, sent_y, got_y, sums,
     pay_send, pay_recv, halo_send, halo_recv, pass_send, pass_recv, link_send, link_recv, own_sem, part_send, part_recv,
 ):
     me = lax.axis_index("space")
@@ -264,9 +264,8 @@
         )
 
     def part_copy(group, target, source):
-        span = pl.ds(group * (moms // groups), moms // groups)
         return remote(
-            src_ref=sent.at[target, span], dst_ref=got.at[source, span],
+            src_ref=(sent, sent_y)[group].at[target], dst_ref=(got, got_y)[group].at[source],
             send_sem=part_send.at[group, target], recv_sem=part_recv.at[group, source], device_id={"space": target},
         )
 
@@ -296,14 +295,25 @@
     column = lambda hop: lax.rem(high + hop, tall)
     beside = [(hop, side) for hop in order for side in (1, 0)][:]
     beside.remove((0, 0))
-    for row in range(per_row):
-        for hop, side in beside:
+    far = sorted(beside, key=lambda hop: -min(hop[0], tall - hop[0]))
+    outer = (high == 0) | (high == tall - 1)
+
+    def send_row(row):
+        for hop, side in far:
             pay_copy(row, 2 * column(hop) + lax.rem(half + side, 2), me).start()
-        if row == 1:
-            for cross, place in enumerate(crossings):
-                @pl.when(me != device_at(place))
-                def _():
-                    halo_copy(cross, me).start()
+
+    send_row(0)
+    send_row(1)
+    for cross, place in enumerate(crossings):
+        @pl.when(me != device_at(place))
+        def _():
+            halo_copy(cross, me).start()
+
+    @pl.when(jnp.logical_not(outer))
+    def _():
+        for row in range(2, per_row):
+            send_row(row)
+
     for row in range(per_row):
         held[row, me] = stage[block, row]
 
@@ -403,20 +413,29 @@
                 jnp.where(quarter == 0, a, b) for a, b in zip(behind[(m - 1) % pieces], behind[m])
             ]
             store_packed(packed, 2 * eigs, first, [f - b for f, b in zip(forward, backward)], row, m)
-        if row:
+        if 0 < row < per_row - 1:
             for m in range(pieces):
                 along_y(pair, first, row - 1, m)
-        if row == per_row - 1:
-            for m in range(pieces):
-                along_y(pair, first, row, m)
-                tails = add_links(links_at(row, m), 18, load_from(held, pair, row, m), -1)
-                store_packed(packed_y, 0, first, [-v for v in tails], row + 1, m)
+
+    def finish_y(pair, carry):
+        first = pl.multiple_of(pair * wide, wide)
+        for m in range(pieces):
+            along_y(pair, first, per_row - 2, m)
+            along_y(pair, first, per_row - 1, m)
+            tails = add_links(links_at(per_row - 1, m), 18, load_from(held, pair, per_row - 1, m), -1)
+            store_packed(packed_y, 0, first, [-v for v in tails], per_row, m)
+        return carry
 
     contract = (((1,), (1,)), ((), ()))
 
     def dot_of(rows, ref, first_row, last_row):
         span = slice(first_row * row_k, last_row * row_k)
-        return lax.dot_general(twisted[rows, span], ref[:, span], contract, preferred_element_type=jnp.float32)
+        middle = (rows.start + rows.stop) // 2
+        parts = [
+            lax.dot_general(twisted[part, span], ref[:, span], contract, preferred_element_type=jnp.float32)
+            for part in (slice(rows.start, middle), slice(middle, rows.stop))
+        ]
+        return jnp.concatenate(parts, axis=0)
 
     every = slice(0, moms * eigs)
     for row in range(per_row):
@@ -431,7 +450,22 @@
             do_row(row, pair)
             return carry
 
-        if row == per_row - 1:
+        lax.fori_loop(0, tall, one, 0)
+        if row + 2 < per_row:
+            @pl.when(outer)
+            def _():
+                send_row(row + 2)
+        if row == 0:
+            @pl.when(jnp.logical_not(after_crossing))
+            def _():
+                pass_copy().start()
+            acc[...] = dot_of(every, packed, 0, 1)
+        if row == 1:
+            acc[...] += dot_of(every, packed, 1, 2)
+            acc_y[...] = dot_of(every, packed_y, 0, 1)
+        if row == 2:
+            acc[...] += dot_of(every, packed, 2, 3)
+        if row == 1:
             @pl.when(at_crossing)
             def _():
                 for step in range(1, count):
@@ -447,41 +481,39 @@
                 return carry
 
             lax.fori_loop(0, tall, last, 0)
-        lax.fori_loop(0, tall, one, 0)
-        if row == 0:
-            @pl.when(jnp.logical_not(after_crossing))
-            def _():
-                pass_copy().start()
-        if row == 1:
-            acc[...] = dot_of(every, packed, 0, 2)
-        if row == 2:
-            acc[...] += dot_of(every, packed, 2, 3)
-            acc_y[...] = dot_of(every, packed_y, 0, 2)
-
-    each = moms // groups
+
     width = 2 * eigs
-    for group in range(groups):
-        rows = slice(group * each * eigs, (group + 1) * each * eigs)
-        along = acc[rows] + dot_of(rows, packed, per_row - 1, per_row)
-        across = acc_y[rows] + dot_of(rows, packed_y, 2, per_row + 1)
-        for d, result in enumerate((along[:, :width], across, along[:, width:])):
-            result = result.reshape(each, count, rows_of, width)
-            for p in range(each):
-                for target in range(count):
-                    sent[target, group * each + p, d] = result[p, target].astype(jnp.bfloat16)
-        for step in range(1, count):
-            part_copy(group, peers(step), me).start()
+
+    def scatter(group, result, index):
+        result = result.reshape(moms, count, rows_of, width)
+        for p in range(moms):
+            for target in range(count):
+                (sent, sent_y)[group][(target, p) + index] = result[p, target].astype(jnp.bfloat16)
+
+    along = acc[...] + dot_of(every, packed, per_row - 1, per_row)
+    for d in range(2):
+        scatter(0, along[:, d * width : (d + 1) * width], (d,))
+    reach = [2 * column(hop) + lax.rem(half + side, 2) for hop, side in far]
+    for target in reach:
+        part_copy(0, target, me).start()
+    lax.fori_loop(0, tall, finish_y, 0)
+    scatter(1, acc_y[...] + dot_of(every, packed_y, 1, per_row + 1), ())
+    for target in reach:
+        part_copy(1, target, me).start()
 
     got[me] = sent[me]
+    got_y[me] = sent_y[me]
     for group in range(groups):
         for step in range(1, count):
             part_copy(group, peers(step), peers(step)).wait_recv()
-        for p in range(group * each, (group + 1) * each):
-            for d in range(NDIR):
-                total = got[0, p, d].astype(jnp.float32)
+        for p in range(moms):
+            for d in range(2 - group):
+                at = (p, d) if group == 0 else (p,)
+                buffer = (got, got_y)[group]
+                total = buffer[(0,) + at].astype(jnp.float32)
                 for source in range(1, count):
-                    total = total + got[source, p, d].astype(jnp.float32)
-                sums[d, p] = total
+                    total = total + buffer[(source,) + at].astype(jnp.float32)
+                sums[2 * d if group == 0 else 1, p] = total
     for d in range(NDIR):
         for p in range(moms):
             out_ref[:, d, p] = sums[directions_ref[d], p]
@@ -516,7 +548,8 @@
     groups = 2
     row_k = 6 * pieces * LANES
     vmem = pl.BlockSpec(memory_space=pltpu.VMEM)
-    part = (count, moms, NDIR, eig_local, 2 * eigs)
+    part = (count, moms, 2, eig_local, 2 * eigs)
+    part_y = (count, moms, eig_local, 2 * eigs)
     lump = (6, pieces, eig_local, LANES)
     summed = pl.pallas_call(
         lambda *refs: kernel(count, depth, groups, *refs),
@@ -543,6 +576,8 @@
             pltpu.VMEM((moms * eigs, 2 * eigs), jnp.float32),
             pltpu.VMEM(part, jnp.bfloat16),
             pltpu.VMEM(part, jnp.bfloat16),
+            pltpu.VMEM(part_y, jnp.bfloat16),
+            pltpu.VMEM(part_y, jnp.bfloat16),
             pltpu.VMEM((NDIR, moms, eig_local, 2 * eigs), jnp.float32),
             pltpu.SemaphoreType.DMA((per_row, count)),
             pltpu.SemaphoreType.DMA((per_row, count)),

time: 45.7 us -> 42.3 us (0.926)
  Pallas kernels: 44 us -> 40.6 us
    pallas_call x1, Pallas kernels: 44 us -> 40.6 us  [shards_by_rows(): pl.pallas_call(lambda *refs: kernel(count, depth, groups, *refs), out_sha...]
where the time goes in v2:
time: 42.3 us; the launch traced here: 42.1 us
  Pallas kernels  40.6 us (96%)
  local copies, waits for them, and re-layouts  1.54 us (4%)
    pallas_call x1, Pallas kernels, shards_by_rows(): pl.pallas_call(lambda *refs: kernel(count, depth, groups, *refs), out_sha...  40.6 us
    unnamed x1, local copies, waits for them, and re-layouts  1.54 us

profile of v2, /device:TPU:0, one launch (start us, length us, event | category | flops | bytes accessed | tf_op | source)
XLA Modules:
  0.0 42.1 jit_solution(13378038218305899409)
XLA Ops:
  0.0 40.6 %elementals.1 = f32[8,3,8,128]{3,2,1,0:T(8,128)} custom-call(bf16[6,8,8,8,128]{4,3,2,1,0:T(8,128)(2,1)} %bitcast.10, bf16[3,18,1024]{2,1,0:T(8,128)(2,1)} %bitcast.12, s32[3,8]{1,0:T(4,128)} %bitcast.13, s32[3]{0:T(128)} %refs_3_.1), custom_call_target="tpu_custom_call" | custom-call | tf_op jit(solution)/shard_map/elementals/pallas_call | solution.py:554
  40.6 1.5 %copy.7 = f32[8,1,8,3,128]{4,2,3,1,0:T(8,128)} copy(f32[8,1,8,3,128]{4,2,3,1,0:T(8,128)} %bitcast.11) | data formatting | bytes 196608

commit v3 on v2

--- a/solution.py
+++ b/solution.py
@@ -591,7 +591,7 @@
             pltpu.SemaphoreType.DMA((groups, count)),
             pltpu.SemaphoreType.DMA((groups, count)),
         ],
-        compiler_params=pltpu.CompilerParams(collective_id=0, has_side_effects=True),
+        compiler_params=pltpu.CompilerParams(collective_id=0, has_side_effects=True, vmem_limit_bytes=55700000),
         name="elementals",
     )(field, gauge_links[0], momenta.T, directions)
     return jnp.transpose(summed, (0, 2, 1, 3))[:, None]

time: 42.3 us -> 42.1 us (level)
  Pallas kernels: 40.6 us -> 39.6 us
  local copies, waits for them, and re-layouts: 1.54 us -> 2.24 us
    pallas_call x1, Pallas kernels: 40.6 us -> 39.6 us  [shards_by_rows(): pl.pallas_call(lambda *refs: kernel(count, depth, groups, *refs), out_sha...]
    unnamed x1 -> x7, local copies, waits for them, and re-layouts: 1.54 us -> 2.24 us
where the time goes in v3:
time: 42.1 us; the launch traced here: 41.9 us
  Pallas kernels  39.6 us (94%)
  local copies, waits for them, and re-layouts  2.24 us (5%)
    pallas_call x1, Pallas kernels, shards_by_rows(): pl.pallas_call(lambda *refs: kernel(count, depth, groups, *refs), out_sha...  39.6 us
    unnamed x7, local copies, waits for them, and re-layouts  2.24 us

profile of v3, /device:TPU:0, one launch (start us, length us, event | category | flops | bytes accessed | tf_op | source)
XLA Modules:
  0.0 41.9 jit_solution(18359000236205874071)
XLA Ops:
  0.0 0.0 copy-start.1
  0.0 0.0 copy-start.2
  0.0 0.7 %copy-done.1 = s32[8,3]{0,1:T(4,128)S(1)} copy-done((s32[8,3]{0,1:T(4,128)S(1)}, s32[8,3]{0,1:T(4,128)}, u32[]{:S(2)}) %copy-start.1) | copy-done | bytes 120
  0.7 0.0 copy-done.2
  0.7 0.0 copy-start
  0.7 0.9 %copy-done = bf16[1,3,18,1024]{3,2,1,0:T(8,128)(2,1)S(1)} copy-done((bf16[1,3,18,1024]{3,2,1,0:T(8,128)(2,1)S(1)}, bf16[1,3,18,1024]{3,2,1,0:T(8,128)(2,1)}, u32[]{:S(2)}) %copy-start) | copy-done | bytes 110616
  1.6 39.6 %elementals.1 = f32[8,3,8,128]{3,2,1,0:T(8,128)S(1)} custom-call(bf16[6,8,8,8,128]{4,3,2,1,0:T(8,128)(2,1)} %bitcast.13, bf16[3,18,1024]{2,1,0:T(8,128)(2,1)S(1)} %bitcast.11, s32[3,8]{1,0:T(4,128)S(1)} %bitcast.12, s32[3]{0:T(128)S(1)} %copy-done.2), custom_call_target="tpu_custom_call" | custom-call | tf_op jit(solution)/shard_map/elementals/pallas_call | solution.py:554
  41.2 0.6 %copy.7 = f32[8,1,8,3,128]{4,2,3,1,0:T(8,128)} copy(f32[8,1,8,3,128]{4,2,3,1,0:T(8,128)S(1)} %bitcast.10) | data formatting | bytes 196608
Async XLA Ops:
  0.0 0.7 %copy-start.1 = (s32[8,3]{0,1:T(4,128)S(1)}, s32[8,3]{0,1:T(4,128)}, u32[]{:S(2)}) copy-start(s32[8,3]{0,1:T(4,128)} %param.6) | copy-start | bytes 292
  0.0 0.7 %copy-start.2 = (s32[3]{0:T(128)S(1)}, s32[3]{0:T(128)}, u32[]{:S(2)}) copy-start(s32[3]{0:T(128)} %refs_3_.1) | copy-start | bytes 40
  0.7 0.9 %copy-start = (bf16[1,3,18,1024]{3,2,1,0:T(8,128)(2,1)S(1)}, bf16[1,3,18,1024]{3,2,1,0:T(8,128)(2,1)}, u32[]{:S(2)}) copy-start(bf16[1,3,18,1024]{3,2,1,0:T(8,128)(2,1)} %param.5) | copy-start | bytes 331780
